TPU v7x, 32 devices: a whole 2x2x4 slice. The times are simulated.
32 devices in a mesh: src: 4 (over z), rcv: 8 (over y, x, core).
Axes of the slice: x: 2, y: 2, z: 4, core: 2. Of those that a mesh axis runs over, the one named last changes fastest.
Arguments:
- traces: bfloat16 [512, 2048, 512], P('src', 'rcv'), may hold values from -6 to 6
- virtual_source_index: int32 [256], replicated, may hold values from 0 to 2047
Outputs:
- correlations: float32 [256, 2048, 512], P('rcv', 'src')
Inputs may be any that keep to these rules, and one draw needn't show every extreme that they name: `virtual_source_index`: receiver numbers; a receiver may be listed more than once.
All inputs are finite; a program needn't handle non-finite values.
Results may differ from a plain program's by a relative error of at most 0.0064.
Values may be sent and summed in bfloat16 or wider, within the bound.
A program may use at most 192 MiB of HBM per device.

v0:
```python
import math

import jax
import jax.numpy as jnp
from jax import lax
from jax.sharding import PartitionSpec as P

NF = 128


def make_tables(times_count):
    freqs = jnp.arange(NF, dtype=jnp.int32)
    times = jnp.arange(times_count, dtype=jnp.int32)
    phase = (freqs[:, None] * times[None, :] % times_count).astype(jnp.float32) * (
        2.0 * math.pi / times_count
    )
    basis = jnp.stack([jnp.cos(phase), -jnp.sin(phase)], axis=1)
    forward = (basis / jnp.sqrt(jnp.float32(times_count))).astype(jnp.bfloat16)
    inverse = (basis / jnp.sqrt(jnp.float32(NF))).astype(jnp.bfloat16)
    return (forward, inverse)


def complex_gram(left_operand, right_operand):
    real_part = jnp.einsum(
        "ekg,ekh->egh", left_operand[:, 0], right_operand[:, 0], preferred_element_type=jnp.float32
    ) + jnp.einsum(
        "ekg,ekh->egh", left_operand[:, 1], right_operand[:, 1], preferred_element_type=jnp.float32
    )
    imaginary_part = jnp.einsum(
        "ekg,ekh->egh", left_operand[:, 0], right_operand[:, 1], preferred_element_type=jnp.float32
    ) - jnp.einsum(
        "ekg,ekh->egh", left_operand[:, 1], right_operand[:, 0], preferred_element_type=jnp.float32
    )
    return jnp.stack([real_part, imaginary_part], axis=1)


def shards(traces, virtual_source_index):
    shots_here, rcv_here, times_count = traces.shape
    forward, inverse = make_tables(times_count)
    spectra = jnp.einsum(
        "kt,srt->ksr",
        forward.reshape(2 * NF, times_count),
        traces,
        preferred_element_type=jnp.float32,
    )
    spectra = spectra.astype(jnp.bfloat16).reshape(NF, 2, shots_here, rcv_here)
    spectra = lax.all_to_all(spectra, "rcv", split_axis=0, concat_axis=3, tiled=True)
    rows = jnp.take(spectra, virtual_source_index, axis=3)
    total_shots = shots_here * lax.axis_size("src")
    columns = lax.all_to_all(spectra, "src", split_axis=3, concat_axis=2, tiled=True)
    gram = complex_gram(lax.all_gather(rows, "src", axis=2, tiled=True), columns)
    scaled = (gram * (1.0 / jnp.sqrt(jnp.float32(total_shots)))).astype(jnp.bfloat16)
    inverse_flattened = inverse.reshape(2 * NF, times_count)
    block = lax.all_to_all(scaled, "rcv", split_axis=2, concat_axis=0, tiled=True)
    folded = block.reshape(2 * NF, block.shape[2], block.shape[3])
    return jnp.einsum("kt,kvr->vrt", inverse_flattened, folded, preferred_element_type=jnp.float32)


def solution(mesh):
    placed = (P("src", "rcv", None), P())
    return jax.shard_map(
        shards, mesh=mesh, in_specs=placed, out_specs=P("rcv", "src", None), check_vma=False
    )
```

profile of v0, /device:TPU:0, one launch (start us, length us, event | category | flops | bytes accessed | tf_op | source)
XLA Modules:
  0.0 1035.7 jit_solution(696779018619299867)
XLA Ops:
  6.5 1.0 sine_negate_fusion
  7.6 0.1 multiply_convert_fusion.1
  7.7 0.3 copy.47
  7.9 0.1 reshape.106
  8.1 19.0 %convolution_convert_fusion = bf16[256,128,256]{2,0,1:T(8,128)(2,1)} fusion(bf16[256,512,1]{1,0,2:T(8,128)(2,1)S(1)} %reshape.106, bf16[128,256,512]{2,1,0:T(8,128)(2,1)} %param.2), kind=kOutput, calls=%fused_computation.3 | convolution fusion | flops 8598323200 | bytes 50593792 | tf_op jit(solution)/shard_map/kt,srt->ksr/dot_general | solution.py:40
  27.0 15.9 %copy.60 = bf16[256,128,256]{2,1,0:T(8,128)(2,1)S(1)} copy(bf16[256,128,256]{2,0,1:T(8,128)(2,1)} %convolution_convert_fusion) | data formatting | bytes 33554432 | tf_op jit(solution)/shard_map/reshape | solution.py:46
  42.9 189.0 %all_to_all.51 = bf16[128,2,128,256]{3,2,1,0:T(8,128)(2,1)} all-to-all(bf16[128,2,128,256]{3,2,1,0:T(8,128)(2,1)S(1)} %bitcast.53), channel_id=1, replica_groups=mesh['src'=4,'rcv'=8] {'rcv'}, dimensions={0} | all-to-all | bytes 33554432 | tf_op jit(solution)/shard_map/all_to_all | solution.py:47
  231.9 21.6 %copy.49 = bf16[16,2,128,8,256]{2,4,3,1,0:T(8,128)(2,1)} copy(bf16[16,2,128,8,256]{4,2,1,0,3:T(8,128)(2,1)} %bitcast.51) | data formatting | bytes 33554432 | tf_op jit(solution)/shard_map/all_to_all | solution.py:47
  253.4 31.0 %copy.52 = bf16[16,2,128,2048]{2,1,0,3:T(2,128)(2,1)} copy(bf16[16,2,128,2048]{2,3,1,0:T(8,128)(2,1)} %bitcast.55) | data formatting | bytes 33554432 | tf_op jit(solution)/shard_map/all_to_all | solution.py:47
  284.4 0.0 copy-start.1
  284.4 7.1 all-to-all-start.1
  291.5 0.2 all-gather.2.cloned.1.call-start
  291.7 0.0 copy-done.1
  291.8 23.3 %copy.61 = bf16[16,2,128,8,256]{2,0,4,3,1:T(8,128)(2,1)} copy(bf16[16,2,128,8,256]{4,2,1,0,3:T(8,128)(2,1)} %bitcast.52) | data formatting | bytes 33554432 | tf_op jit(solution)/shard_map/all_to_all | solution.py:47
  315.1 6.8 gather_fusion
  322.0 2.4 fusion.7
  324.4 0.0 all-gather.2.cloned.1.call-update
  324.4 464.7 %all-to-all-done.1 = bf16[16,2,128,2048]{2,1,0,3:T(2,128)(2,1)} async-done(((bf16[16,2,128,2048]{2,1,0,3:T(2,128)(2,1)}), bf16[16,2,128,2048]{2,1,0,3:T(2,128)(2,1)}, u32[]{:S(2)}, u32[]{:S(2)}) %all-to-all-start.1) | async-done | bytes 16777248 | tf_op jit(solution)/shard_map/all_to_all | solution.py:50
  789.1 15.2 %copy.53 = bf16[16,2,128,2048]{2,3,1,0:T(8,128)(2,1)} copy(bf16[16,2,128,2048]{2,1,0,3:T(2,128)(2,1)} %all-to-all-done.1) | data formatting | bytes 33554432 | tf_op jit(solution)/shard_map/all_to_all | solution.py:50
  804.2 22.4 %copy.54 = bf16[16,2,4,128,512]{4,3,2,0,1:T(8,128)(2,1)} copy(bf16[16,2,4,128,512]{3,4,2,1,0:T(8,128)(2,1)} %bitcast.54) | data formatting | bytes 33554432 | tf_op jit(solution)/shard_map/all_to_all | solution.py:50
  826.6 0.0 all-gather.2.cloned.1.call-done
  826.6 0.0 copy-start
  826.6 11.4 %fusion.3 = f32[16,256,512]{2,1,0:T(8,128)} fusion(bf16[16,2,512,512]{3,2,0,1:T(8,128)(2,1)} %bitcast.47, bf16[16,2,512,256]{2,3,0,1:T(8,128)(2,1)} %all-gather.2.cloned.1.call-done), kind=kOutput, calls=%fused_computation.10 | convolution fusion | flops 2147483648 | bytes 20971520 | tf_op jit(solution)/shard_map/ekg,ekh->egh/dot_general | solution.py:31
  838.0 1.0 copy-done
  839.1 6.8 fusion.4
  845.9 9.3 subtract_bitcast_fusion
  855.2 12.7 %add_bitcast_fusion = f32[16,1,256,512]{3,2,0,1:T(8,128)} fusion(f32[16,256,512]{2,1,0:T(8,128)} %fusion.4, bf16[16,2,512,512]{3,2,0,1:T(8,128)(2,1)} %bitcast.49, bf16[16,2,512,256]{2,3,0,1:T(8,128)(2,1)} %all-gather.2.cloned.1.call-done), kind=kOutput, calls=%fused_computation.9 | convolution fusion | flops 2149580800 | bytes 29360128 | tf_op jit(solution)/shard_map/ekg,ekh->egh/dot_general | solution.py:26
  867.9 8.1 fusion
  876.1 11.5 %copy.55 = bf16[16,2,256,512]{3,0,1,2:T(8,128)(2,1)} copy(bf16[16,2,256,512]{3,2,0,1:T(8,128)(2,1)} %fusion) | data formatting | bytes 16777216 | tf_op jit(solution)/shard_map/convert_element_type | solution.py:52
  887.6 4.9 all-to-all-start.2
  892.6 0.3 copy.58
  892.8 0.1 reshape.107
  892.9 93.6 %all-to-all-done.2 = bf16[16,2,256,512]{3,0,1,2:T(8,128)(2,1)} async-done(((bf16[16,2,256,512]{3,0,1,2:T(8,128)(2,1)}), bf16[16,2,256,512]{3,0,1,2:T(8,128)(2,1)}, u32[]{:S(2)}, u32[]{:S(2)}) %all-to-all-start.2) | async-done | bytes 8388640 | tf_op jit(solution)/shard_map/all_to_all | solution.py:54
  986.6 11.9 %copy.57 = bf16[8,16,2,32,512]{4,3,2,1,0:T(8,128)(2,1)} copy(bf16[8,16,2,32,512]{4,1,2,3,0:T(8,128)(2,1)} %bitcast.17) | data formatting | bytes 16777216 | tf_op jit(solution)/shard_map/all_to_all | solution.py:54
  998.5 29.9 %fusion.1 = f32[32,512,512]{2,1,0:T(8,128)} fusion(bf16[256,512,1]{1,0,2:T(8,128)(2,1)S(1)} %reshape.107, bf16[256,32,512]{2,1,0:T(8,128)(2,1)} %bitcast.56), kind=kOutput, calls=%fused_computation.6 | convolution fusion | flops 4294967296 | bytes 42205184 | tf_op jit(solution)/shard_map/kt,kvr->vrt/dot_general | solution.py:56
  (3 shorter events, 0.0 us)
Async XLA Ops:
  284.4 7.4 copy-start.1
  284.4 504.7 %all-to-all-start.1 = ((bf16[16,2,128,2048]{2,1,0,3:T(2,128)(2,1)}), bf16[16,2,128,2048]{2,1,0,3:T(2,128)(2,1)}, u32[]{:S(2)}, u32[]{:S(2)}) async-start(bf16[16,2,128,2048]{2,1,0,3:T(2,128)(2,1)} %copy.52), calls=%async_computation.1 | async-start | bytes 33554432 | tf_op jit(solution)/shard_map/all_to_all | solution.py:50
  291.5 535.1 %all-gather.2.cloned.1.call-start = ((), (), s32[]{:S(2)}) async-start(), calls=%async_computation.3 | async-start | bytes 10485760 | tf_op jit(solution)/shard_map/all_gather | solution.py:51
  826.6 12.4 %copy-start = (bf16[16,2,4,128,512]{4,3,2,0,1:T(8,128)(2,1)S(1)}, bf16[16,2,4,128,512]{4,3,2,0,1:T(8,128)(2,1)}, u32[]{:S(2)}) copy-start(bf16[16,2,4,128,512]{4,3,2,0,1:T(8,128)(2,1)} %copy.54) | copy-start | bytes 50331652
  887.6 99.0 %all-to-all-start.2 = ((bf16[16,2,256,512]{3,0,1,2:T(8,128)(2,1)}), bf16[16,2,256,512]{3,0,1,2:T(8,128)(2,1)}, u32[]{:S(2)}, u32[]{:S(2)}) async-start(bf16[16,2,256,512]{3,0,1,2:T(8,128)(2,1)} %copy.55), calls=%async_computation.2 | async-start | bytes 16777216 | tf_op jit(solution)/shard_map/all_to_all | solution.py:54
Sparse Core Ops, SparseCore 0:
  324.5 300.9 all-gather.1
where the time goes:
time: 1040 us
  waiting for transfers between devices  558 us (54%)
  blocking collectives  189 us (18%)
  local copies, waits for them, and re-layouts  161 us (15%)
  matrix products  89.1 us (9%)
  between operations  14 us (1%)
  starting transfers between devices  12.3 us (1%)
  other arithmetic  11.7 us (1%)
    all_to_all x1, waiting for transfers between devices, shards(): lax.all_to_all(spectra, 'src', split_axis=3, concat_axis=2, tiled=True)  465 us
    all_to_all x1, blocking collectives, shards(): lax.all_to_all(spectra, 'rcv', split_axis=0, concat_axis=3, tiled=True)  189 us
    all_to_all x1, waiting for transfers between devices, shards(): lax.all_to_all(scaled, 'rcv', split_axis=2, concat_axis=0, tiled=True)  93.6 us
    all_to_all x3, local copies, waits for them, and re-layouts, shards(): lax.all_to_all(spectra, 'rcv', split_axis=0, concat_axis=3, tiled=True)  75.9 us
    all_to_all x2, local copies, waits for them, and re-layouts, shards(): lax.all_to_all(spectra, 'src', split_axis=3, concat_axis=2, tiled=True)  37.6 us
    dot_general x1, matrix products, shards(): jnp.einsum('kt,kvr->vrt', inverse_flattened, folded, preferred_element_ty...  29.9 us
  transfers between devices with their start and end apart: 3, of which 2 were waited for; matrix products, arithmetic and copies ran while one was open for 7% of the time, Pallas kernels for 0%

commit v1 on v0

v1 whole, which is shorter than its diff:
```python
import functools
import math

import jax
import jax.numpy as jnp
from jax import lax
from jax.experimental import pallas as pl
from jax.sharding import PartitionSpec as P


NF = 128
CHUNKS = 4


def make_tables(times_count):
    freqs = jnp.arange(NF, dtype=jnp.int32)
    times = jnp.arange(times_count, dtype=jnp.int32)
    phase = (freqs[:, None] * times[None, :] % times_count).astype(jnp.float32) * (
        2.0 * math.pi / times_count
    )
    basis = jnp.stack([jnp.cos(phase), -jnp.sin(phase)], axis=1)
    forward = (basis / jnp.sqrt(jnp.float32(times_count))).astype(jnp.bfloat16)
    inverse = (basis / jnp.sqrt(jnp.float32(NF))).astype(jnp.bfloat16)
    return (forward, inverse)


def rows_kernel(spectra_ref, pick_ref, rows_ref):
    owners, _, _, shots, receivers = spectra_ref.shape
    total = None
    for owner in range(owners):
        part = jnp.dot(
            spectra_ref[owner, 0].reshape(2 * shots, receivers),
            pick_ref[owner],
            preferred_element_type=jnp.float32,
        )
        total = part if total is None else total + part
    rows_ref[0] = total.astype(rows_ref.dtype).reshape(rows_ref.shape[1:])


def pick_rows(spectra, pick):
    owners, freqs, _, shots, receivers = spectra.shape
    sources = pick.shape[2]
    return pl.pallas_call(
        rows_kernel,
        grid=(freqs,),
        in_specs=[
            pl.BlockSpec((owners, 1, 2, shots, receivers), lambda f: (0, f, 0, 0, 0)),
            pl.BlockSpec((owners, receivers, sources), lambda f: (0, 0, 0)),
        ],
        out_specs=pl.BlockSpec((1, 2, shots, sources), lambda f: (f, 0, 0, 0)),
        out_shape=jax.ShapeDtypeStruct((freqs, 2, shots, sources), jnp.bfloat16),
        cost_estimate=pl.CostEstimate(
            flops=4 * freqs * shots * owners * receivers * sources,
            bytes_accessed=spectra.size * 2 + pick.size * 2,
            transcendentals=0,
        ),
    )(spectra, pick)


def gram_kernel(scale, groups, *refs):
    rows_refs, columns_refs, out_ref = refs[:groups], refs[groups:-1], refs[-1]
    _, _, shots, sources = rows_refs[0].shape
    blocks, receivers = columns_refs[0].shape[0], columns_refs[0].shape[4]
    rows = [rows_ref[0] for rows_ref in rows_refs]
    real_left = jnp.concatenate([row.reshape(2 * shots, sources) for row in rows], axis=0)
    imaginary_left = jnp.concatenate(
        [piece for row in rows for piece in (-row[1], row[0])], axis=0
    )
    owners, _, _, own, _ = out_ref.shape
    for block in range(blocks):
        right = jnp.concatenate(
            [
                columns_ref[block, 0].reshape(2 * shots, receivers)
                for columns_ref in columns_refs
            ],
            axis=0,
        )
        for part, left in enumerate((real_left, imaginary_left)):
            gram = lax.dot_general(
                left, right, (((0,), (0,)), ((), ())), preferred_element_type=jnp.float32
            )
            out_ref[:, 0, part, :, block * receivers : (block + 1) * receivers] = (
                (gram * scale).astype(out_ref.dtype).reshape(owners, own, receivers)
            )


def scaled_gram(rows, columns, owners):
    groups = len(rows)
    freqs, _, shots, sources = rows[0].shape
    blocks, receivers = columns[0].shape[0], columns[0].shape[4]
    own = sources // owners
    scale = 1.0 / math.sqrt(groups * shots)
    return pl.pallas_call(
        functools.partial(gram_kernel, scale, groups),
        grid=(freqs,),
        in_specs=[pl.BlockSpec((1, 2, shots, sources), lambda f: (f, 0, 0, 0))] * groups
        + [pl.BlockSpec((blocks, 1, 2, shots, receivers), lambda f: (0, f, 0, 0, 0))]
        * groups,
        out_specs=pl.BlockSpec(
            (owners, 1, 2, own, blocks * receivers), lambda f: (0, f, 0, 0, 0)
        ),
        out_shape=jax.ShapeDtypeStruct(
            (owners, freqs, 2, own, blocks * receivers), jnp.bfloat16
        ),
        cost_estimate=pl.CostEstimate(
            flops=8 * freqs * groups * shots * sources * blocks * receivers,
            bytes_accessed=groups * (rows[0].size + columns[0].size) * 2,
            transcendentals=0,
        ),
    )(*rows, *columns)


def shifted(array, shift, count):
    return lax.ppermute(array, "src", [(i, (i + shift) % count) for i in range(count)])


def shards(traces, virtual_source_index):
    shots_here, rcv_here, times_count = traces.shape
    n_src, n_rcv = lax.axis_size("src"), lax.axis_size("rcv")
    me = lax.axis_index("src")
    sources = virtual_source_index.shape[0]
    forward, inverse = make_tables(times_count)
    chunks = CHUNKS
    per = NF // n_rcv // chunks
    forward = forward.reshape(n_rcv, chunks, per, 2, times_count)
    inverse = inverse.reshape(n_rcv, chunks, per, 2, times_count)
    receivers = jnp.arange(n_rcv * rcv_here, dtype=jnp.int32)
    pick = (receivers[:, None] == virtual_source_index[None, :]).astype(jnp.bfloat16)
    pick = pick.reshape(n_rcv, rcv_here, sources)
    blocks = n_rcv // n_src
    folded = []
    for chunk in range(chunks):
        spectra = jnp.einsum(
            "kt,srt->ksr",
            forward[:, chunk].reshape(n_rcv * per * 2, times_count),
            traces,
            preferred_element_type=jnp.float32,
        )
        spectra = spectra.astype(jnp.bfloat16)
        spectra = spectra.reshape(n_rcv, per, 2, shots_here, rcv_here)
        spectra = lax.all_to_all(
            spectra, "rcv", split_axis=0, concat_axis=0, tiled=True
        )
        columns = spectra.reshape(n_src, blocks, per, 2, shots_here, rcv_here)
        pieces = []
        for shift in range(n_src):
            target = lax.rem(me + shift, n_src)
            piece = lax.dynamic_index_in_dim(columns, target, 0, keepdims=False)
            pieces.append(shifted(piece, shift, n_src) if shift else piece)
        rows = pick_rows(spectra, pick)
        rows = [shifted(rows, shift, n_src) if shift else rows for shift in range(n_src)]
        scaled = scaled_gram(rows, pieces, n_rcv)
        folded.append(
            lax.all_to_all(scaled, "rcv", split_axis=0, concat_axis=0, tiled=True)
        )
    folded = jnp.stack(folded, axis=1)
    folded = folded.reshape(NF * 2, folded.shape[4], folded.shape[5])
    return jnp.einsum(
        "kt,kvr->vrt",
        inverse.reshape(NF * 2, times_count),
        folded,
        preferred_element_type=jnp.float32,
    )


def solution(mesh):
    placed = (P("src", "rcv", None), P())

    return jax.shard_map(
        shards, mesh=mesh, in_specs=placed, out_specs=P("rcv", "src", None), check_vma=False
    )
```

time: 1040 us -> 899 us (0.86)
  blocking collectives: 189 us -> 0 us
  local copies, waits for them, and re-layouts: 161 us -> 51.6 us
  starting transfers between devices: 12.3 us -> 70.4 us
  waiting for transfers between devices: 558 us -> 616 us
  Pallas kernels: 0 us -> 45.1 us
  between operations: 14 us -> 0.66 us
    ppermute x0 -> x24, waiting for transfers between devices: none -> 506 us  [shifted(): lax.ppermute(array, 'src', [(i, (i + shift) % count) for i in range(count)])]
    all_to_all x2 -> x8, waiting for transfers between devices: 558 us -> 110 us  [the longest x4 84.4 us: shards(): lax.all_to_all(spectra, 'rcv', split_axis=0, concat_axis=0, tiled=True)]
    all_to_all x1 -> x0, blocking collectives: 189 us -> none  [shards(): lax.all_to_all(spectra, 'rcv', split_axis=0, concat_axis=3, tiled=True)]
    all_to_all x6 -> x0, local copies, waits for them, and re-layouts: 125 us -> none  [the longest x3 75.9 us: shards(): lax.all_to_all(spectra, 'rcv', split_axis=0, concat_axis=3, tiled=True)]
    pallas_call x0 -> x8, Pallas kernels: none -> 45.1 us  [the longest x4 25 us: scaled_gram(): pl.pallas_call(functools.partial(gram_kernel, scale, groups), grid=(freqs...]
    ppermute x0 -> x24, starting transfers between devices: none -> 34 us  [shifted(): lax.ppermute(array, 'src', [(i, (i + shift) % count) for i in range(count)])]
    all_to_all x2 -> x8, starting transfers between devices: 12.1 us -> 36.4 us  [the longest x4 19.5 us: shards(): lax.all_to_all(spectra, 'rcv', split_axis=0, concat_axis=0, tiled=True)]
    reshape x1 -> x0, local copies, waits for them, and re-layouts: 15.9 us -> none  [shards(): spectra = spectra.astype(jnp.bfloat16).reshape(NF, 2, shots_here, rcv_here)]
  transfers between devices with their start and end apart: 3 -> 32, of which waited for: 2 -> 12; matrix products, arithmetic and copies ran while one was open for 7% -> 9% of each run, Pallas kernels for 0% -> 5%
where the time goes in v1:
time: 899 us; the launch traced here: 889 us
  waiting for transfers between devices  616 us (69%)
  matrix products  95.6 us (11%)
  starting transfers between devices  70.4 us (8%)
  local copies, waits for them, and re-layouts  51.6 us (6%)
  Pallas kernels  45.1 us (5%)
  other arithmetic  10.2 us (1%)
    ppermute x24, waiting for transfers between devices, shifted(): lax.ppermute(array, 'src', [(i, (i + shift) % count) for i in range(count)])  506 us
    all_to_all x4, waiting for transfers between devices, shards(): lax.all_to_all(spectra, 'rcv', split_axis=0, concat_axis=0, tiled=True)  84.4 us
    dot_general x4, matrix products, shards(): jnp.einsum('kt,srt->ksr', forward[:, chunk].reshape(n_rcv * per * 2, time...  65.8 us
    ppermute x24, starting transfers between devices, shifted(): lax.ppermute(array, 'src', [(i, (i + shift) % count) for i in range(count)])  34 us
    dot_general x1, matrix products, shards(): jnp.einsum('kt,kvr->vrt', inverse.reshape(NF * 2, times_count), folded, p...  29.9 us
    all_to_all x4, waiting for transfers between devices, shards(): lax.all_to_all(scaled, 'rcv', split_axis=0, concat_axis=0, tiled=True)  25.1 us
    pallas_call x4, Pallas kernels, scaled_gram(): pl.pallas_call(functools.partial(gram_kernel, scale, groups), grid=(freqs...  25 us
    pallas_call x4, Pallas kernels, pick_rows(): pl.pallas_call(rows_kernel, grid=(freqs,), in_specs=[pl.BlockSpec((owners...  20.1 us
  transfers between devices with their start and end apart: 32, of which 12 were waited for; matrix products, arithmetic and copies ran while one was open for 9% of the time, Pallas kernels for 5%

profile of v1, /device:TPU:0, one launch (start us, length us, event | category | flops | bytes accessed | tf_op | source)
XLA Modules:
  0.0 889.2 jit_solution(11912472981561845487)
XLA Ops:
  1.3 16.4 %convolution_convert_fusion.2 = bf16[64,128,256]{2,0,1:T(8,128)(2,1)S(1)} fusion(bf16[64,512,1]{1,0,2:T(8,128)(2,1)S(1)} %reshape.173, bf16[128,256,512]{2,1,0:T(8,128)(2,1)} %param.2), kind=kOutput, calls=%fused_computation.5 | convolution fusion | flops 2149580800 | bytes 37814272 | tf_op jit(solution)/shard_map/kt,srt->ksr/dot_general | solution.py:133
  17.7 4.4 copy.22
  22.2 5.2 all-to-all-start.2
  27.5 16.4 %convolution_convert_fusion.1 = bf16[64,128,256]{2,0,1:T(8,128)(2,1)S(1)} fusion(bf16[64,512,1]{1,0,2:T(8,128)(2,1)S(1)} %reshape.174, bf16[128,256,512]{2,1,0:T(8,128)(2,1)} %param.2), kind=kOutput, calls=%fused_computation.4 | convolution fusion | flops 2149580800 | bytes 37814272 | tf_op jit(solution)/shard_map/kt,srt->ksr/dot_general | solution.py:133
  43.9 4.4 copy.24
  48.4 28.2 %all-to-all-done.2.spectra_ref = bf16[8,4,2,128,256]{4,3,2,1,0:T(8,128)(2,1)} async-done(((bf16[8,4,2,128,256]{4,3,2,1,0:T(8,128)(2,1)}), bf16[8,4,2,128,256]{4,3,2,1,0:T(8,128)(2,1)}, u32[]{:S(2)}, u32[]{:S(2)}) %all-to-all-start.2) | async-done | bytes 4194336 | tf_op jit(solution)/shard_map/all_to_all | solution.py:141
  76.6 5.1 all-to-all-start.4
  81.7 16.4 %convolution_convert_fusion.3 = bf16[64,128,256]{2,0,1:T(8,128)(2,1)S(1)} fusion(bf16[64,512,1]{1,0,2:T(8,128)(2,1)S(1)} %reshape.172, bf16[128,256,512]{2,1,0:T(8,128)(2,1)} %param.2), kind=kOutput, calls=%fused_computation.6 | convolution fusion | flops 2149580800 | bytes 37814272 | tf_op jit(solution)/shard_map/kt,srt->ksr/dot_general | solution.py:133
  98.2 4.5 copy.20
  102.7 28.0 %all-to-all-done.4.spectra_ref = bf16[8,4,2,128,256]{4,3,2,1,0:T(8,128)(2,1)} async-done(((bf16[8,4,2,128,256]{4,3,2,1,0:T(8,128)(2,1)}), bf16[8,4,2,128,256]{4,3,2,1,0:T(8,128)(2,1)}, u32[]{:S(2)}, u32[]{:S(2)}) %all-to-all-start.4) | async-done | bytes 4194336 | tf_op jit(solution)/shard_map/all_to_all | solution.py:141
  130.7 4.6 all-to-all-start
  135.4 16.4 %convolution_convert_fusion = bf16[64,128,256]{2,0,1:T(8,128)(2,1)S(1)} fusion(bf16[64,512,1]{1,0,2:T(8,128)(2,1)S(1)} %reshape.175, bf16[128,256,512]{2,1,0:T(8,128)(2,1)} %param.2), kind=kOutput, calls=%fused_computation.3 | convolution fusion | flops 2149580800 | bytes 37814272 | tf_op jit(solution)/shard_map/kt,srt->ksr/dot_general | solution.py:133
  151.9 4.4 copy.26
  156.3 28.1 %all-to-all-done.spectra_ref = bf16[8,4,2,128,256]{4,3,2,1,0:T(8,128)(2,1)} async-done(((bf16[8,4,2,128,256]{4,3,2,1,0:T(8,128)(2,1)}), bf16[8,4,2,128,256]{4,3,2,1,0:T(8,128)(2,1)}, u32[]{:S(2)}, u32[]{:S(2)}) %all-to-all-start) | async-done | bytes 4194336 | tf_op jit(solution)/shard_map/all_to_all | solution.py:141
  184.4 4.7 all-to-all-start.6
  190.5 5.0 shard_map.28.refs_0_
  195.5 4.4 collective-permute-start.2
  199.9 3.7 dynamic-slice_bitcast_fusion.12
  205.6 2.9 collective-permute-start.1
  208.6 4.0 collective-permute-done.2.refs_3_
  213.0 122.2 %collective-permute-done.1.refs_2_ = bf16[4,2,128,256]{3,2,1,0:T(8,128)(2,1)S(1)} collective-permute-done((bf16[4,2,128,256]{3,2,1,0:T(8,128)(2,1)S(1)}, bf16[4,2,128,256]{3,2,1,0:T(8,128)(2,1)S(1)}, u32[]{:S(2)}, u32[]{:S(2)}) %collective-permute-start.1) | collective-permute-done | bytes 524320 | tf_op jit(solution)/shard_map/ppermute | solution.py:114
  337.3 6.2 shard_map.29
  343.5 3.9 all-to-all-start.1
  347.4 5.0 shard_map.34.refs_0_
  352.4 3.7 dynamic-slice_bitcast_fusion
  356.1 4.9 collective-permute-start.23
  363.9 3.5 collective-permute-done.20.refs_3_
  369.3 122.8 %collective-permute-done.19.refs_2_ = bf16[4,2,128,256]{3,2,1,0:T(8,128)(2,1)S(1)} collective-permute-done((bf16[4,2,128,256]{3,2,1,0:T(8,128)(2,1)S(1)}, bf16[4,2,128,256]{3,2,1,0:T(8,128)(2,1)S(1)}, u32[]{:S(2)}, u32[]{:S(2)}) %collective-permute-start.19) | collective-permute-done | bytes 524320 | tf_op jit(solution)/shard_map/ppermute | solution.py:114
  494.8 6.2 shard_map.35
  501.1 4.4 all-to-all-start.7
  505.4 5.0 shard_map.32.refs_0_
  510.5 3.7 dynamic-slice_bitcast_fusion.4
  515.2 2.5 collective-permute-start.16
  519.2 6.3 collective-permute-done.14.refs_3_
  525.5 120.8 %collective-permute-done.13.refs_2_ = bf16[4,2,128,256]{3,2,1,0:T(8,128)(2,1)S(1)} collective-permute-done((bf16[4,2,128,256]{3,2,1,0:T(8,128)(2,1)S(1)}, bf16[4,2,128,256]{3,2,1,0:T(8,128)(2,1)S(1)}, u32[]{:S(2)}, u32[]{:S(2)}) %collective-permute-start.13) | collective-permute-done | bytes 524320 | tf_op jit(solution)/shard_map/ppermute | solution.py:114
  649.0 6.2 shard_map.33
  655.2 4.3 all-to-all-start.5
  659.6 5.0 shard_map.30.refs_0_
  664.6 3.7 dynamic-slice_bitcast_fusion.8
  668.4 4.8 collective-permute-start.11
  676.1 3.6 collective-permute-done.8.refs_3_
  681.5 122.7 %collective-permute-done.7.refs_2_ = bf16[4,2,128,256]{3,2,1,0:T(8,128)(2,1)S(1)} collective-permute-done((bf16[4,2,128,256]{3,2,1,0:T(8,128)(2,1)S(1)}, bf16[4,2,128,256]{3,2,1,0:T(8,128)(2,1)S(1)}, u32[]{:S(2)}, u32[]{:S(2)}) %collective-permute-start.7) | collective-permute-done | bytes 524320 | tf_op jit(solution)/shard_map/ppermute | solution.py:114
  806.8 6.2 shard_map.31
  813.1 4.4 all-to-all-start.3
  818.9 25.1 %all-to-all-done.3 = bf16[8,4,2,32,512]{4,3,2,1,0:T(8,128)(2,1)} async-done(((bf16[8,4,2,32,512]{4,3,2,1,0:T(8,128)(2,1)}), bf16[8,4,2,32,512]{4,3,2,1,0:T(8,128)(2,1)}, u32[]{:S(2)}, u32[]{:S(2)}) %all-to-all-start.3) | async-done | bytes 2097184 | tf_op jit(solution)/shard_map/all_to_all | solution.py:154
  844.1 6.6 pad_maximum_fusion
  850.7 8.4 copy.27
  859.1 29.9 %fusion = f32[32,512,512]{2,1,0:T(8,128)} fusion(bf16[256,512,1]{1,0,2:T(8,128)(2,1)S(1)} %reshape.176, bf16[256,32,512]{2,1,0:T(8,128)(2,1)} %bitcast.62), kind=kOutput, calls=%fused_computation.1 | convolution fusion | flops 4294967296 | bytes 42205184 | tf_op jit(solution)/shard_map/kt,kvr->vrt/dot_general | solution.py:158
  (115 shorter events, 28.8 us)
Async XLA Ops:
  22.2 54.4 %all-to-all-start.2 = ((bf16[8,4,2,128,256]{4,3,2,1,0:T(8,128)(2,1)}), bf16[8,4,2,128,256]{4,3,2,1,0:T(8,128)(2,1)}, u32[]{:S(2)}, u32[]{:S(2)}) async-start(bf16[8,4,2,128,256]{4,3,2,1,0:T(8,128)(2,1)} %bitcast.66), calls=%async_computation.2 | async-start | bytes 8388608 | tf_op jit(solution)/shard_map/all_to_all | solution.py:141
  76.6 54.2 %all-to-all-start.4 = ((bf16[8,4,2,128,256]{4,3,2,1,0:T(8,128)(2,1)}), bf16[8,4,2,128,256]{4,3,2,1,0:T(8,128)(2,1)}, u32[]{:S(2)}, u32[]{:S(2)}) async-start(bf16[8,4,2,128,256]{4,3,2,1,0:T(8,128)(2,1)} %bitcast.65), calls=%async_computation.4 | async-start | bytes 8388608 | tf_op jit(solution)/shard_map/all_to_all | solution.py:141
  130.7 53.7 %all-to-all-start = ((bf16[8,4,2,128,256]{4,3,2,1,0:T(8,128)(2,1)}), bf16[8,4,2,128,256]{4,3,2,1,0:T(8,128)(2,1)}, u32[]{:S(2)}, u32[]{:S(2)}) async-start(bf16[8,4,2,128,256]{4,3,2,1,0:T(8,128)(2,1)} %bitcast.64), calls=%async_computation | async-start | bytes 8388608 | tf_op jit(solution)/shard_map/all_to_all | solution.py:141
  184.4 4.7 copy-start.28
  184.4 159.1 %all-to-all-start.6 = ((bf16[8,4,2,128,256]{4,3,2,1,0:T(8,128)(2,1)}), bf16[8,4,2,128,256]{4,3,2,1,0:T(8,128)(2,1)}, u32[]{:S(2)}, u32[]{:S(2)}) async-start(bf16[8,4,2,128,256]{4,3,2,1,0:T(8,128)(2,1)} %bitcast.63), calls=%async_computation.6 | async-start | bytes 8388608 | tf_op jit(solution)/shard_map/all_to_all | solution.py:141
  195.5 17.1 %collective-permute-start.2 = (bf16[4,2,128,256]{3,2,1,0:T(8,128)(2,1)}, bf16[4,2,128,256]{3,2,1,0:T(8,128)(2,1)S(1)}, u32[]{:S(2)}, u32[]{:S(2)}) collective-permute-start(bf16[4,2,128,256]{3,2,1,0:T(8,128)(2,1)} %shard_map.28.refs_0_), channel_id=1, source_target_pairs={{0,24},{8,0},{16,8},{24,16},{1,25},{9,1},{17,9},{25,17},{2,26},{10... | collective-permute-start | bytes 1572872 | tf_op jit(solution)/shard_map/ppermute | solution.py:114
  199.9 5.7 copy-start.1
  203.6 131.7 %collective-permute-start.5 = (bf16[2,4,2,128,256]{4,3,2,1,0:T(8,128)(2,1)S(1)}, bf16[2,4,2,128,256]{4,3,2,1,0:T(8,128)(2,1)S(1)}, u32[]{:S(2)}, u32[]{:S(2)}) collective-permute-start(bf16[2,4,2,128,256]{4,3,2,1,0:T(8,128)(2,1)S(1)} %get-tuple-element.5), channel_id=1, source_target_pairs={{0,24},{8,0},{16,8},{24,16},{1,25},{9,1},{17,9},{25,17},{2,26},{10... | collective-permute-start | bytes 3145736 | tf_op jit(solution)/shard_map/ppermute | solution.py:114
  204.1 131.2 %collective-permute-start.4 = (bf16[2,4,2,128,256]{4,3,2,1,0:T(8,128)(2,1)S(1)}, bf16[2,4,2,128,256]{4,3,2,1,0:T(8,128)(2,1)S(1)}, u32[]{:S(2)}, u32[]{:S(2)}) collective-permute-start(bf16[2,4,2,128,256]{4,3,2,1,0:T(8,128)(2,1)S(1)} %get-tuple-element.6), channel_id=1, source_target_pairs={{0,16},{8,24},{16,0},{24,8},{1,17},{9,25},{17,1},{25,9},{2,18},{10... | collective-permute-start | bytes 3145736 | tf_op jit(solution)/shard_map/ppermute | solution.py:114
  204.1 131.3 %collective-permute-start.3 = (bf16[2,4,2,128,256]{4,3,2,1,0:T(8,128)(2,1)S(1)}, bf16[2,4,2,128,256]{4,3,2,1,0:T(8,128)(2,1)S(1)}, u32[]{:S(2)}, u32[]{:S(2)}) collective-permute-start(bf16[2,4,2,128,256]{4,3,2,1,0:T(8,128)(2,1)S(1)} %get-tuple-element.7), channel_id=1, source_target_pairs={{0,8},{8,16},{16,24},{24,0},{1,9},{9,17},{17,25},{25,1},{2,10},{10... | collective-permute-start | bytes 3145736 | tf_op jit(solution)/shard_map/ppermute | solution.py:114
  205.6 129.6 %collective-permute-start.1 = (bf16[4,2,128,256]{3,2,1,0:T(8,128)(2,1)S(1)}, bf16[4,2,128,256]{3,2,1,0:T(8,128)(2,1)S(1)}, u32[]{:S(2)}, u32[]{:S(2)}) collective-permute-start(bf16[4,2,128,256]{3,2,1,0:T(8,128)(2,1)S(1)} %copy-done.1), channel_id=1, source_target_pairs={{0,16},{8,24},{16,0},{24,8},{1,17},{9,25},{17,1},{25,9},{2,18},{10... | collective-permute-start | bytes 1572872 | tf_op jit(solution)/shard_map/ppermute | solution.py:114
  212.6 124.6 %copy-start.17 = (bf16[4,2,128,256]{3,2,1,0:T(8,128)(2,1)}, bf16[4,2,128,256]{3,2,1,0:T(8,128)(2,1)S(1)}, u32[]{:S(2)}) copy-start(bf16[4,2,128,256]{3,2,1,0:T(8,128)(2,1)S(1)} %collective-permute-done.2.refs_3_) | copy-start | bytes 1572868
  212.6 122.7 %collective-permute-start = (bf16[4,2,128,256]{3,2,1,0:T(8,128)(2,1)S(1)}, bf16[4,2,128,256]{3,2,1,0:T(8,128)(2,1)S(1)}, u32[]{:S(2)}, u32[]{:S(2)}) collective-permute-start(bf16[4,2,128,256]{3,2,1,0:T(8,128)(2,1)S(1)} %copy-done.1), channel_id=1, source_target_pairs={{0,8},{8,16},{16,24},{24,0},{1,9},{9,17},{17,25},{25,1},{2,10},{10... | collective-permute-start | bytes 1572872 | tf_op jit(solution)/shard_map/ppermute | solution.py:114
  335.3 2.0 copy-start.4
  335.3 2.0 copy-start.8
  343.5 157.6 %all-to-all-start.1 = ((bf16[8,4,2,32,512]{4,3,2,1,0:T(8,128)(2,1)}), bf16[8,4,2,32,512]{4,3,2,1,0:T(8,128)(2,1)S(1)}, u32[]{:S(2)}, u32[]{:S(2)}) async-start(bf16[8,4,2,32,512]{4,3,2,1,0:T(8,128)(2,1)} %shard_map.29), calls=%async_computation.1 | async-start | bytes 4194304 | tf_op jit(solution)/shard_map/all_to_all | solution.py:154
  352.4 15.0 %collective-permute-start.20 = (bf16[4,2,128,256]{3,2,1,0:T(8,128)(2,1)}, bf16[4,2,128,256]{3,2,1,0:T(8,128)(2,1)S(1)}, u32[]{:S(2)}, u32[]{:S(2)}) collective-permute-start(bf16[4,2,128,256]{3,2,1,0:T(8,128)(2,1)} %shard_map.34.refs_0_), channel_id=1, source_target_pairs={{0,24},{8,0},{16,8},{24,16},{1,25},{9,1},{17,9},{25,17},{2,26},{10... | collective-permute-start | bytes 1572872 | tf_op jit(solution)/shard_map/ppermute | solution.py:114
  352.4 9.1 %copy-start.2 = (bf16[4,2,128,256]{3,2,1,0:T(8,128)(2,1)S(1)}, bf16[4,2,128,256]{3,2,1,0:T(8,128)(2,1)}, u32[]{:S(2)}) copy-start(bf16[4,2,128,256]{3,2,1,0:T(8,128)(2,1)} %shard_map.34.refs_0_) | copy-start | bytes 1572868
  356.1 136.1 %collective-permute-start.23 = (bf16[2,4,2,128,256]{4,3,2,1,0:T(8,128)(2,1)S(1)}, bf16[2,4,2,128,256]{4,3,2,1,0:T(8,128)(2,1)S(1)}, u32[]{:S(2)}, u32[]{:S(2)}) collective-permute-start(bf16[2,4,2,128,256]{4,3,2,1,0:T(8,128)(2,1)S(1)} %get-tuple-element.17), channel_id=1, source_target_pairs={{0,24},{8,0},{16,8},{24,16},{1,25},{9,1},{17,9},{25,17},{2,26},{10... | collective-permute-start | bytes 3145736 | tf_op jit(solution)/shard_map/ppermute | solution.py:114
  361.0 131.2 %collective-permute-start.22 = (bf16[2,4,2,128,256]{4,3,2,1,0:T(8,128)(2,1)S(1)}, bf16[2,4,2,128,256]{4,3,2,1,0:T(8,128)(2,1)S(1)}, u32[]{:S(2)}, u32[]{:S(2)}) collective-permute-start(bf16[2,4,2,128,256]{4,3,2,1,0:T(8,128)(2,1)S(1)} %get-tuple-element.18), channel_id=1, source_target_pairs={{0,16},{8,24},{16,0},{24,8},{1,17},{9,25},{17,1},{25,9},{2,18},{10... | collective-permute-start | bytes 3145736 | tf_op jit(solution)/shard_map/ppermute | solution.py:114
  361.0 131.3 %collective-permute-start.21 = (bf16[2,4,2,128,256]{4,3,2,1,0:T(8,128)(2,1)S(1)}, bf16[2,4,2,128,256]{4,3,2,1,0:T(8,128)(2,1)S(1)}, u32[]{:S(2)}, u32[]{:S(2)}) collective-permute-start(bf16[2,4,2,128,256]{4,3,2,1,0:T(8,128)(2,1)S(1)} %get-tuple-element.19), channel_id=1, source_target_pairs={{0,8},{8,16},{16,24},{24,0},{1,9},{9,17},{17,25},{25,1},{2,10},{10... | collective-permute-start | bytes 3145736 | tf_op jit(solution)/shard_map/ppermute | solution.py:114
  361.5 130.6 %collective-permute-start.19 = (bf16[4,2,128,256]{3,2,1,0:T(8,128)(2,1)S(1)}, bf16[4,2,128,256]{3,2,1,0:T(8,128)(2,1)S(1)}, u32[]{:S(2)}, u32[]{:S(2)}) collective-permute-start(bf16[4,2,128,256]{3,2,1,0:T(8,128)(2,1)S(1)} %copy-done.2), channel_id=1, source_target_pairs={{0,16},{8,24},{16,0},{24,8},{1,17},{9,25},{17,1},{25,9},{2,18},{10... | collective-permute-start | bytes 1572872 | tf_op jit(solution)/shard_map/ppermute | solution.py:114
  367.4 127.4 %copy-start.18 = (bf16[4,2,128,256]{3,2,1,0:T(8,128)(2,1)}, bf16[4,2,128,256]{3,2,1,0:T(8,128)(2,1)S(1)}, u32[]{:S(2)}) copy-start(bf16[4,2,128,256]{3,2,1,0:T(8,128)(2,1)S(1)} %collective-permute-done.20.refs_3_) | copy-start | bytes 1572868
  367.4 124.8 %collective-permute-start.18 = (bf16[4,2,128,256]{3,2,1,0:T(8,128)(2,1)S(1)}, bf16[4,2,128,256]{3,2,1,0:T(8,128)(2,1)S(1)}, u32[]{:S(2)}, u32[]{:S(2)}) collective-permute-start(bf16[4,2,128,256]{3,2,1,0:T(8,128)(2,1)S(1)} %copy-done.2), channel_id=1, source_target_pairs={{0,8},{8,16},{16,24},{24,0},{1,9},{9,17},{17,25},{25,1},{2,10},{10... | collective-permute-start | bytes 1572872 | tf_op jit(solution)/shard_map/ppermute | solution.py:114
  492.2 1.6 copy-start.9
  501.1 154.2 %all-to-all-start.7 = ((bf16[8,4,2,32,512]{4,3,2,1,0:T(8,128)(2,1)}), bf16[8,4,2,32,512]{4,3,2,1,0:T(8,128)(2,1)}, u32[]{:S(2)}, u32[]{:S(2)}) async-start(bf16[8,4,2,32,512]{4,3,2,1,0:T(8,128)(2,1)} %shard_map.35), calls=%async_computation.7 | async-start | bytes 4194304 | tf_op jit(solution)/shard_map/all_to_all | solution.py:154
  510.5 15.0 %collective-permute-start.14 = (bf16[4,2,128,256]{3,2,1,0:T(8,128)(2,1)}, bf16[4,2,128,256]{3,2,1,0:T(8,128)(2,1)S(1)}, u32[]{:S(2)}, u32[]{:S(2)}) collective-permute-start(bf16[4,2,128,256]{3,2,1,0:T(8,128)(2,1)} %shard_map.32.refs_0_), channel_id=1, source_target_pairs={{0,24},{8,0},{16,8},{24,16},{1,25},{9,1},{17,9},{25,17},{2,26},{10... | collective-permute-start | bytes 1572872 | tf_op jit(solution)/shard_map/ppermute | solution.py:114
  510.5 7.2 copy-start.3
  514.2 132.1 %collective-permute-start.17 = (bf16[2,4,2,128,256]{4,3,2,1,0:T(8,128)(2,1)S(1)}, bf16[2,4,2,128,256]{4,3,2,1,0:T(8,128)(2,1)S(1)}, u32[]{:S(2)}, u32[]{:S(2)}) collective-permute-start(bf16[2,4,2,128,256]{4,3,2,1,0:T(8,128)(2,1)S(1)} %get-tuple-element.13), channel_id=1, source_target_pairs={{0,24},{8,0},{16,8},{24,16},{1,25},{9,1},{17,9},{25,17},{2,26},{10... | collective-permute-start | bytes 3145736 | tf_op jit(solution)/shard_map/ppermute | solution.py:114
  515.2 131.1 %collective-permute-start.16 = (bf16[2,4,2,128,256]{4,3,2,1,0:T(8,128)(2,1)S(1)}, bf16[2,4,2,128,256]{4,3,2,1,0:T(8,128)(2,1)S(1)}, u32[]{:S(2)}, u32[]{:S(2)}) collective-permute-start(bf16[2,4,2,128,256]{4,3,2,1,0:T(8,128)(2,1)S(1)} %get-tuple-element.14), channel_id=1, source_target_pairs={{0,16},{8,24},{16,0},{24,8},{1,17},{9,25},{17,1},{25,9},{2,18},{10... | collective-permute-start | bytes 3145736 | tf_op jit(solution)/shard_map/ppermute | solution.py:114
  517.7 128.6 %collective-permute-start.15 = (bf16[2,4,2,128,256]{4,3,2,1,0:T(8,128)(2,1)S(1)}, bf16[2,4,2,128,256]{4,3,2,1,0:T(8,128)(2,1)S(1)}, u32[]{:S(2)}, u32[]{:S(2)}) collective-permute-start(bf16[2,4,2,128,256]{4,3,2,1,0:T(8,128)(2,1)S(1)} %get-tuple-element.15), channel_id=1, source_target_pairs={{0,8},{8,16},{16,24},{24,0},{1,9},{9,17},{17,25},{25,1},{2,10},{10... | collective-permute-start | bytes 3145736 | tf_op jit(solution)/shard_map/ppermute | solution.py:114
  517.7 128.6 %collective-permute-start.13 = (bf16[4,2,128,256]{3,2,1,0:T(8,128)(2,1)S(1)}, bf16[4,2,128,256]{3,2,1,0:T(8,128)(2,1)S(1)}, u32[]{:S(2)}, u32[]{:S(2)}) collective-permute-start(bf16[4,2,128,256]{3,2,1,0:T(8,128)(2,1)S(1)} %copy-done.3), channel_id=1, source_target_pairs={{0,16},{8,24},{16,0},{24,8},{1,17},{9,25},{17,1},{25,9},{2,18},{10... | collective-permute-start | bytes 1572872 | tf_op jit(solution)/shard_map/ppermute | solution.py:114
  525.5 123.5 %copy-start.19 = (bf16[4,2,128,256]{3,2,1,0:T(8,128)(2,1)}, bf16[4,2,128,256]{3,2,1,0:T(8,128)(2,1)S(1)}, u32[]{:S(2)}) copy-start(bf16[4,2,128,256]{3,2,1,0:T(8,128)(2,1)S(1)} %collective-permute-done.14.refs_3_) | copy-start | bytes 1572868
  525.5 120.8 %collective-permute-start.12 = (bf16[4,2,128,256]{3,2,1,0:T(8,128)(2,1)S(1)}, bf16[4,2,128,256]{3,2,1,0:T(8,128)(2,1)S(1)}, u32[]{:S(2)}, u32[]{:S(2)}) collective-permute-start(bf16[4,2,128,256]{3,2,1,0:T(8,128)(2,1)S(1)} %copy-done.3), channel_id=1, source_target_pairs={{0,8},{8,16},{16,24},{24,0},{1,9},{9,17},{17,25},{25,1},{2,10},{10... | collective-permute-start | bytes 1572872 | tf_op jit(solution)/shard_map/ppermute | solution.py:114
  646.3 1.4 copy-start.6
  646.3 1.7 copy-start.10
  655.2 157.8 %all-to-all-start.5 = ((bf16[8,4,2,32,512]{4,3,2,1,0:T(8,128)(2,1)}), bf16[8,4,2,32,512]{4,3,2,1,0:T(8,128)(2,1)}, u32[]{:S(2)}, u32[]{:S(2)}) async-start(bf16[8,4,2,32,512]{4,3,2,1,0:T(8,128)(2,1)} %shard_map.33), calls=%async_computation.5 | async-start | bytes 4194304 | tf_op jit(solution)/shard_map/all_to_all | solution.py:154
  664.6 15.0 %collective-permute-start.8 = (bf16[4,2,128,256]{3,2,1,0:T(8,128)(2,1)}, bf16[4,2,128,256]{3,2,1,0:T(8,128)(2,1)S(1)}, u32[]{:S(2)}, u32[]{:S(2)}) collective-permute-start(bf16[4,2,128,256]{3,2,1,0:T(8,128)(2,1)} %shard_map.30.refs_0_), channel_id=1, source_target_pairs={{0,24},{8,0},{16,8},{24,16},{1,25},{9,1},{17,9},{25,17},{2,26},{10... | collective-permute-start | bytes 1572872 | tf_op jit(solution)/shard_map/ppermute | solution.py:114
  664.6 9.1 %copy-start = (bf16[4,2,128,256]{3,2,1,0:T(8,128)(2,1)S(1)}, bf16[4,2,128,256]{3,2,1,0:T(8,128)(2,1)}, u32[]{:S(2)}) copy-start(bf16[4,2,128,256]{3,2,1,0:T(8,128)(2,1)} %shard_map.30.refs_0_) | copy-start | bytes 1572868
  668.4 135.8 %collective-permute-start.11 = (bf16[2,4,2,128,256]{4,3,2,1,0:T(8,128)(2,1)S(1)}, bf16[2,4,2,128,256]{4,3,2,1,0:T(8,128)(2,1)S(1)}, u32[]{:S(2)}, u32[]{:S(2)}) collective-permute-start(bf16[2,4,2,128,256]{4,3,2,1,0:T(8,128)(2,1)S(1)} %get-tuple-element.9), channel_id=1, source_target_pairs={{0,24},{8,0},{16,8},{24,16},{1,25},{9,1},{17,9},{25,17},{2,26},{10... | collective-permute-start | bytes 3145736 | tf_op jit(solution)/shard_map/ppermute | solution.py:114
  673.1 131.1 %collective-permute-start.10 = (bf16[2,4,2,128,256]{4,3,2,1,0:T(8,128)(2,1)S(1)}, bf16[2,4,2,128,256]{4,3,2,1,0:T(8,128)(2,1)S(1)}, u32[]{:S(2)}, u32[]{:S(2)}) collective-permute-start(bf16[2,4,2,128,256]{4,3,2,1,0:T(8,128)(2,1)S(1)} %get-tuple-element.10), channel_id=1, source_target_pairs={{0,16},{8,24},{16,0},{24,8},{1,17},{9,25},{17,1},{25,9},{2,18},{10... | collective-permute-start | bytes 3145736 | tf_op jit(solution)/shard_map/ppermute | solution.py:114
  673.1 131.1 %collective-permute-start.9 = (bf16[2,4,2,128,256]{4,3,2,1,0:T(8,128)(2,1)S(1)}, bf16[2,4,2,128,256]{4,3,2,1,0:T(8,128)(2,1)S(1)}, u32[]{:S(2)}, u32[]{:S(2)}) collective-permute-start(bf16[2,4,2,128,256]{4,3,2,1,0:T(8,128)(2,1)S(1)} %get-tuple-element.11), channel_id=1, source_target_pairs={{0,8},{8,16},{16,24},{24,0},{1,9},{9,17},{17,25},{25,1},{2,10},{10... | collective-permute-start | bytes 3145736 | tf_op jit(solution)/shard_map/ppermute | solution.py:114
  673.7 130.5 %collective-permute-start.7 = (bf16[4,2,128,256]{3,2,1,0:T(8,128)(2,1)S(1)}, bf16[4,2,128,256]{3,2,1,0:T(8,128)(2,1)S(1)}, u32[]{:S(2)}, u32[]{:S(2)}) collective-permute-start(bf16[4,2,128,256]{3,2,1,0:T(8,128)(2,1)S(1)} %copy-done), channel_id=1, source_target_pairs={{0,16},{8,24},{16,0},{24,8},{1,17},{9,25},{17,1},{25,9},{2,18},{10... | collective-permute-start | bytes 1572872 | tf_op jit(solution)/shard_map/ppermute | solution.py:114
  679.6 127.2 %copy-start.16 = (bf16[4,2,128,256]{3,2,1,0:T(8,128)(2,1)}, bf16[4,2,128,256]{3,2,1,0:T(8,128)(2,1)S(1)}, u32[]{:S(2)}) copy-start(bf16[4,2,128,256]{3,2,1,0:T(8,128)(2,1)S(1)} %collective-permute-done.8.refs_3_) | copy-start | bytes 1572868
  679.6 124.5 %collective-permute-start.6 = (bf16[4,2,128,256]{3,2,1,0:T(8,128)(2,1)S(1)}, bf16[4,2,128,256]{3,2,1,0:T(8,128)(2,1)S(1)}, u32[]{:S(2)}, u32[]{:S(2)}) collective-permute-start(bf16[4,2,128,256]{3,2,1,0:T(8,128)(2,1)S(1)} %copy-done), channel_id=1, source_target_pairs={{0,8},{8,16},{16,24},{24,0},{1,9},{9,17},{17,25},{25,1},{2,10},{10... | collective-permute-start | bytes 1572872 | tf_op jit(solution)/shard_map/ppermute | solution.py:114
  804.2 1.3 copy-start.7
  804.2 1.6 copy-start.11
  813.1 31.0 %all-to-all-start.3 = ((bf16[8,4,2,32,512]{4,3,2,1,0:T(8,128)(2,1)}), bf16[8,4,2,32,512]{4,3,2,1,0:T(8,128)(2,1)}, u32[]{:S(2)}, u32[]{:S(2)}) async-start(bf16[8,4,2,32,512]{4,3,2,1,0:T(8,128)(2,1)} %shard_map.31), calls=%async_computation.3 | async-start | bytes 4194304 | tf_op jit(solution)/shard_map/all_to_all | solution.py:154
  (13 other events, 12.4 us)
